TPU v7x, 256 devices: a whole 4x4x8 slice. The times are simulated.
256 devices in a mesh: row: 8 (over z), col: 32 (over y, x, core).
Axes of the slice: x: 4, y: 4, z: 8, core: 2. Of those that a mesh axis runs over, the one named last changes fastest.
Arguments:
- factor: bfloat16 [131072, 5, 1024], P('col', None, 'row'), may hold values from -0.0625 to 0.0625
- diag_inverse: bfloat16 [5, 1024, 1024], P(None, 'row'), may hold values from -1 to 2
- right_side: float32 [16, 128, 1024], P(None, 'col', 'row'), may hold values from -6 to 6
- tile_order: int32 [128], replicated, may hold values from 0 to 127, each once
- live_segments: int32 [16], replicated, may hold values from 2 to 5
Outputs:
- result: float32 [16, 128, 1024], P(None, 'col', 'row')
Inputs may be any that keep to these rules, and one draw needn't show every extreme that they name: `tile_order`: each of 0 to 127 appears once.
All inputs are finite; a program needn't handle non-finite values.
Results may differ from a plain program's by a relative error of at most 0.0019.
Values may be sent and summed in bfloat16 or wider, within the bound.
No kernel may reach another device: no remote copies, remote signals or barrier semaphores. Data moves between devices by JAX's collectives and lax.ppermute only.
A program may use at most 64 MiB of HBM per device.

v0:
```python
import functools

import jax
import jax.numpy as jnp
from jax import lax
from jax.experimental import pallas as pl
from jax.experimental.pallas import tpu as pltpu
from jax.sharding import PartitionSpec as P


NT = (((1,), (1,)), ((), ()))
F32 = jnp.float32
BF16 = jnp.bfloat16
CHIP, PLACE, MINE = 2, 3, 8


def to_all(array, axis, peers, groups=None):
    copies = jnp.broadcast_to(array[None], (peers, *array.shape))
    return lax.all_to_all(copies, axis, 0, 0, axis_index_groups=groups, tiled=True)


def from_mask(array, mask):
    size = lax.axis_size("col")
    return lax.ppermute(array, "col", [(i, i ^ mask) for i in range(size)])


def levels(size):
    bits = size.bit_length() - 1
    return [(low, min(2, bits - low)) for low in range(1, bits, 2)][::-1]


def moved_by_mask(array, parts):
    for (low, bits), part in zip(levels(lax.axis_size("col")), parts, strict=True):
        branches = [lambda value: value]
        for step in range(1, 1 << bits):
            branches.append(functools.partial(from_mask, mask=step << low))
        array = lax.switch(part, branches, array)
    return array


def window_kernel(at_ref, *refs):
    count = len(refs) // 2
    for rows_ref, out_ref in zip(refs[:count], refs[count:], strict=True):
        out_ref[...] = rows_ref[...]


def window_rows(at, factor, section_count, tile_width):
    width = factor.shape[2]

    def spec(section, index_map):
        return pl.BlockSpec((section, tile_width, width), index_map)

    later = range(1, section_count)
    return pl.pallas_call(
        window_kernel,
        out_shape=[jax.ShapeDtypeStruct((t, tile_width, width), factor.dtype) for t in later],
        grid_spec=pltpu.PrefetchScalarGridSpec(
            num_scalar_prefetch=1,
            grid=(1,),
            in_specs=[spec(t, lambda i, at, t=t: (0, at[PLACE + t], 0)) for t in later],
            out_specs=[spec(t, lambda i, at: (0, 0, 0)) for t in later],
        ),
        compiler_params=pltpu.CompilerParams(vmem_limit_bytes=14 << 20),
        cost_estimate=pl.CostEstimate(flops=0, bytes_accessed=5 << 20, transcendentals=0),
    )(at, *[factor for _ in later])


def partial_kernel(section, at_ref, sent_ref, own_ref, other_ref, own_side, other_side, out_ref):
    me, core = at_ref[0], at_ref[1]
    peers, half, _ = out_ref.shape
    width = own_side.shape[2]
    columns = pl.ds(pl.multiple_of(me * width, width), width)

    def write(rows_ref, side_ref):
        total = lax.dot_general(sent_ref[0], rows_ref[0], NT, preferred_element_type=F32)
        for before in range(1, section):
            total = total + lax.dot_general(
                sent_ref[before], rows_ref[before], NT, preferred_element_type=F32
            )
        value = -jnp.where(core == 0, total[:half], total[half:])
        side = jnp.where(core == 0, side_ref[0, :half], side_ref[0, half:])
        for peer in range(peers):
            out_ref[peer] = value
            out_ref[peer, :, columns] = out_ref[peer, :, columns] + side

    mine = at_ref[MINE + section]

    @pl.when(mine == 1)
    def _():
        write(own_ref, own_side)

    @pl.when(mine != 1)
    def _():
        write(other_ref, other_side)


def partial_half(section, at, sent, own_rows, other_rows, own_sides, other_sides, peers):
    _, rhs_count, width = sent.shape
    tile_width = own_rows.shape[1]
    half = rhs_count // 2
    rows = pl.BlockSpec((section, tile_width, width), lambda i, at: (0, 0, 0))
    side = pl.BlockSpec((1, rhs_count, width), lambda i, at: (section, 0, 0))
    return pl.pallas_call(
        functools.partial(partial_kernel, section),
        out_shape=jax.ShapeDtypeStruct((peers, half, tile_width), F32),
        grid_spec=pltpu.PrefetchScalarGridSpec(
            num_scalar_prefetch=1,
            grid=(1,),
            in_specs=[
                pl.BlockSpec((section, rhs_count, width), lambda i, at: (0, 0, 0)),
                rows,
                rows,
                side,
                side,
            ],
            out_specs=pl.BlockSpec((peers, half, tile_width), lambda i, at: (0, 0, 0)),
        ),
        compiler_params=pltpu.CompilerParams(vmem_limit_bytes=8 << 20),
        cost_estimate=pl.CostEstimate(
            flops=2 * section * rhs_count * width * tile_width,
            bytes_accessed=4 * section * width * tile_width,
            transcendentals=0,
        ),
    )(at, sent, own_rows, other_rows, own_sides, other_sides)


def trailing_kernel(at_ref, sent_ref, rows_ref, out_ref):
    total = lax.dot_general(sent_ref[0, 0], rows_ref[0], NT, preferred_element_type=F32)
    for before in range(1, rows_ref.shape[0]):
        total = total + lax.dot_general(
            sent_ref[0, before], rows_ref[before], NT, preferred_element_type=F32
        )
    width = out_ref.shape[3]
    for peer in range(out_ref.shape[0]):
        out_ref[peer, 0] = total[:, peer * width : (peer + 1) * width]


def trailing(at, sent, factor, tile_width, peers):
    _, count, rhs_count, width = sent.shape
    tiles = factor.shape[1] // tile_width
    return pl.pallas_call(
        trailing_kernel,
        out_shape=jax.ShapeDtypeStruct((peers, tiles, rhs_count, width), F32),
        grid_spec=pltpu.PrefetchScalarGridSpec(
            num_scalar_prefetch=1,
            grid=(tiles,),
            in_specs=[
                pl.BlockSpec((1, count, rhs_count, width), lambda i, at: (at[CHIP], 0, 0, 0)),
                pl.BlockSpec((count, tile_width, width), lambda i, at: (0, i, 0)),
            ],
            out_specs=pl.BlockSpec((peers, 1, rhs_count, width), lambda i, at: (0, i, 0, 0)),
        ),
        compiler_params=pltpu.CompilerParams(vmem_limit_bytes=10 << 20),
        cost_estimate=pl.CostEstimate(
            flops=2 * count * rhs_count * width * tile_width * tiles,
            bytes_accessed=2 * count * width * tile_width * tiles,
            transcendentals=0,
        ),
    )(at, sent, factor)


def per_device(factor, diag_inverse, right_side, tile_order, live_segments):
    section_count, slice_width, tile_width = diag_inverse.shape
    rhs_count, rows_dev, _ = right_side.shape
    half = rhs_count // 2
    peers = tile_width // slice_width
    cols = lax.axis_size("col")
    my_col, me = lax.axis_index("col"), lax.axis_index("row")
    core = my_col & 1
    factor = jnp.transpose(factor, (1, 0, 2))
    slots = tile_order[:section_count]
    owner = lax.div(slots, jnp.int32(rows_dev))
    place = lax.rem(slots, jnp.int32(rows_dev))
    local = jnp.arange(rows_dev, dtype=jnp.int32)
    order = jnp.arange(section_count, dtype=jnp.int32)
    here = place[:, None] == local[None, :]
    sides = jnp.where(here[:, None, :, None], right_side[None], 0.0).sum(axis=2)
    mine = owner == my_col

    def own_half(array):
        return jnp.where(core == 0, array[:half], array[half:])

    other_sides = from_mask(sides, 1)
    share = own_half(jnp.where(mine[0], sides[0], other_sides[0]))
    arrived = to_all(share, "row", peers)

    chip = lax.shift_right_logical(owner[-1], jnp.int32(1))
    head = jnp.stack([me, core, chip])
    at = jnp.concatenate([head, place, mine.astype(jnp.int32)]).astype(jnp.int32)
    own_rows = window_rows(at, factor, section_count, tile_width)
    other_rows = [from_mask(rows, 1) for rows in own_rows]
    masks = owner[1:] ^ owner[:-1]
    parts = [
        lax.shift_right_logical(masks, jnp.int32(low)) & ((1 << bits) - 1)
        for low, bits in levels(cols)
    ]
    live = order[:, None] < live_segments[None, :]
    taken = (here & mine[:, None])[:, None, :] & live[:, :, None]
    done = taken.any(axis=0)[:, :, None]
    first = (arrived, at, live, taken, done, sides, other_sides, own_rows, other_rows)
    arrived, at, live, taken, done, sides, other_sides, own_rows, other_rows = (
        lax.optimization_barrier(first)
    )

    remaining = jnp.moveaxis(arrived, 0, 1).reshape(half, tile_width)
    history = None
    solves = []
    for section in range(section_count):
        if section:
            copies = partial_half(
                section,
                at,
                history,
                own_rows[section - 1],
                other_rows[section - 1],
                sides,
                other_sides,
                peers,
            )
            copies, history, solves = lax.optimization_barrier((copies, history, solves))
            remaining = lax.all_to_all(copies, "row", 0, 0, tiled=True).sum(axis=0)
        solved = lax.dot_general(
            remaining,
            diag_inverse[section].astype(F32),
            NT,
            precision=lax.Precision.HIGHEST,
            preferred_element_type=F32,
        )
        other = from_mask(solved, 1)
        solved = jnp.where(
            core == 0, jnp.concatenate([solved, other]), jnp.concatenate([other, solved])
        )
        solves.append(solved)
        sent = jnp.where(live[section][:, None], solved, 0.0).astype(BF16)[None]
        history = sent if history is None else jnp.concatenate([history, sent])
        if section < section_count - 1:
            history, solves = lax.optimization_barrier((history, solves))
            history = moved_by_mask(history, [part[section] for part in parts])
    result = jnp.where(taken[..., None], jnp.stack(solves)[:, :, None, :], 0.0).sum(axis=0)
    history, result = lax.optimization_barrier((history, result))
    planes = [list(range(first, cols, 2)) for first in range(2)]
    everywhere = to_all(history, "col", cols // 2, planes)
    pieces = trailing(at, everywhere, factor, tile_width, peers)
    total = lax.all_to_all(pieces, "row", 0, 0, tiled=True).sum(axis=0)
    updated = right_side - jnp.moveaxis(total, 0, 1)
    return jnp.where(done, result, updated)


def solution(mesh):
    return jax.shard_map(
        per_device,
        mesh=mesh,
        in_specs=(P("col", None, "row"), P(None, "row", None), P(None, "col", "row"), P(), P()),
        out_specs=P(None, "col", "row"),
        check_vma=False,
    )
```

profile of v0, /device:TPU:1, one launch (start us, length us, event | category | flops | bytes accessed | tf_op | source)
XLA Modules:
  0.0 166.6 jit_solution(14595797110032599191)
XLA Ops:
  2.3 3.3 %collective-permute-start.24 = (f32[5,16,128]{2,1,0:T(8,128)S(1)}, f32[5,16,128]{2,1,0:T(8,128)S(1)}, u32[]{:S(2)}, u32[]{:S(2)}) collective-permute-start(f32[5,16,128]{2,1,0:T(8,128)S(1)} %select_reduce_fusion.1.own_side), channel_id=1, source_target_pairs={{0,1},{1,0},{2,3},{3,2},{4,5},{5,4},{6,7},{7,6},{8,9},{9,8},{10,11... | collective-permute-start | bytes 122888 | tf_op jit(solution)/shard_map/ppermute | solution.py:24
  12.6 6.5 %all-to-all-start = ((f32[8,8,128]{2,1,0:T(8,128)}), f32[8,8,128]{2,1,0:T(8,128)S(1)}, u32[]{:S(2)}, u32[]{:S(2)}) async-start(f32[8,8,128]{2,1,0:T(8,128)} %broadcast_in_dim.118), calls=%async_computation | async-start | bytes 65536 | tf_op jit(solution)/shard_map/all_to_all | solution.py:19
  21.1 4.9 %all-to-all-done = f32[8,8,128]{2,1,0:T(8,128)S(1)} async-done(((f32[8,8,128]{2,1,0:T(8,128)}), f32[8,8,128]{2,1,0:T(8,128)S(1)}, u32[]{:S(2)}, u32[]{:S(2)}) %all-to-all-start) | async-done | bytes 32800 | tf_op jit(solution)/shard_map/all_to_all | solution.py:19
  29.6 4.0 %conditional.8 = (bf16[1,16,128]{2,1,0:T(8,128)(2,1)S(1)}) conditional(s32[]{:T(128)} %bitcast.14, bf16[1,16,128]{2,1,0:T(8,128)(2,1)S(1)} %fusion.18, bf16[1,16,128]{2,1,0:T(8,128)(2,1)S(1)} %fusion.18, bf16[1,16,128]{2,1,0:T(8,128)(2,1)S(1)} %fusion.18, bf16[1,16,128]{2,1,0:T(8,128)(2,1)S(1)} %fusion.18), branch_computations={%region_2.3_spmd, %region_3.4_spmd, %region_4.5_spmd, %region_5.6_... | conditional | bytes 24624 | solution.py:37
  29.6 3.0 %collective-permute-start.1 = (bf16[1,16,128]{2,1,0:T(8,128)(2,1)S(1)}, bf16[1,16,128]{2,1,0:T(8,128)(2,1)S(1)}, u32[]{:S(2)}, u32[]{:S(2)}) collective-permute-start(bf16[1,16,128]{2,1,0:T(8,128)(2,1)S(1)} %param.2), channel_id=1, source_target_pairs={{0,16},{1,17},{2,18},{3,19},{4,20},{5,21},{6,22},{7,23},{8,24},{9,... | collective-permute-start | bytes 12296 | tf_op jit(solution)/shard_map/cond/branch_2_fun/ppermute | solution.py:24
  35.4 13.3 %all_to_all.35 = f32[8,8,1024]{2,1,0:T(8,128)} all-to-all(f32[8,8,1024]{2,1,0:T(8,128)S(1)} %shard_map.56), channel_id=1, replica_groups=mesh['row'=8,'col'=32] {'row'}, dimensions={0} | all-to-all | bytes 524288 | tf_op jit(solution)/shard_map/all_to_all | solution.py:221
  51.0 2.6 %collective-permute-start.30 = (f32[8,128]{1,0:T(8,128)S(1)}, f32[8,128]{1,0:T(8,128)S(1)}, u32[]{:S(2)}, u32[]{:S(2)}) collective-permute-start(f32[8,128]{1,0:T(8,128)S(1)} %fusion.6), channel_id=1, source_target_pairs={{0,1},{1,0},{2,3},{3,2},{4,5},{5,4},{6,7},{7,6},{8,9},{9,8},{10,11... | collective-permute-start | bytes 12296 | tf_op jit(solution)/shard_map/ppermute | solution.py:24
  55.6 2.6 %conditional.10 = (bf16[2,16,128]{2,1,0:T(8,128)(2,1)S(1)}) conditional(s32[]{:T(128)} %bitcast.12, bf16[2,16,128]{2,1,0:T(8,128)(2,1)S(1)} %pad_maximum_fusion.3, bf16[2,16,128]{2,1,0:T(8,128)(2,1)S(1)} %pad_maximum_fusion.3, bf16[2,16,128]{2,1,0:T(8,128)(2,1)S(1)} %pad_maximum_fusion.3, ...), branch_computations={%region_11.12_spmd, %region_12.13_spmd, %region_13.14_spmd, %regio... | conditional | bytes 49200 | solution.py:37
  58.2 4.0 %conditional.11 = (bf16[2,16,128]{2,1,0:T(8,128)(2,1)S(1)}) conditional(s32[]{:T(128)} %bitcast.11, bf16[2,16,128]{2,1,0:T(8,128)(2,1)S(1)} %get-tuple-element.211, bf16[2,16,128]{2,1,0:T(8,128)(2,1)S(1)} %get-tuple-element.211, bf16[2,16,128]{2,1,0:T(8,128)(2,1)S(1)} %get-tuple-element.211, ...), branch_computations={%region_15.16_spmd, %region_16.17_spmd, %region_17.18_spmd, %regio... | conditional | bytes 49200 | solution.py:37
  58.2 2.7 %collective-permute-start.10 = (bf16[2,16,128]{2,1,0:T(8,128)(2,1)S(1)}, bf16[2,16,128]{2,1,0:T(8,128)(2,1)S(1)}, u32[]{:S(2)}, u32[]{:S(2)}) collective-permute-start(bf16[2,16,128]{2,1,0:T(8,128)(2,1)S(1)} %param.14), channel_id=1, source_target_pairs={{0,4},{1,5},{2,6},{3,7},{4,0},{5,1},{6,2},{7,3},{8,12},{9,13},{10,... | collective-permute-start | bytes 24584 | tf_op jit(solution)/shard_map/cond/branch_2_fun/ppermute | solution.py:24
  64.1 11.9 %all_to_all.36 = f32[8,8,1024]{2,1,0:T(8,128)S(1)} all-to-all(f32[8,8,1024]{2,1,0:T(8,128)S(1)} %shard_map.57), channel_id=1, replica_groups=mesh['row'=8,'col'=32] {'row'}, dimensions={0} | all-to-all | bytes 524288 | tf_op jit(solution)/shard_map/all_to_all | solution.py:221
  77.3 3.4 %collective-permute-start.31 = (f32[8,128]{1,0:T(8,128)S(1)}, f32[8,128]{1,0:T(8,128)S(1)}, u32[]{:S(2)}, u32[]{:S(2)}) collective-permute-start(f32[8,128]{1,0:T(8,128)S(1)} %fusion.4), channel_id=1, source_target_pairs={{0,1},{1,0},{2,3},{3,2},{4,5},{5,4},{6,7},{7,6},{8,9},{9,8},{10,11... | collective-permute-start | bytes 12296 | tf_op jit(solution)/shard_map/ppermute | solution.py:24
  82.0 3.9 %conditional.13 = (bf16[3,16,128]{2,1,0:T(8,128)(2,1)S(1)}) conditional(s32[]{:T(128)} %bitcast.9, bf16[3,16,128]{2,1,0:T(8,128)(2,1)S(1)} %get-tuple-element.213, bf16[3,16,128]{2,1,0:T(8,128)(2,1)S(1)} %get-tuple-element.213, bf16[3,16,128]{2,1,0:T(8,128)(2,1)S(1)} %get-tuple-element.213, ...), branch_computations={%region_24.25_spmd, %region_25.26_spmd, %region_26.27_spmd, %regio... | conditional | bytes 73776 | solution.py:37
  87.9 12.7 %all_to_all.37 = f32[8,8,1024]{2,1,0:T(8,128)S(1)} all-to-all(f32[8,8,1024]{2,1,0:T(8,128)S(1)} %shard_map.58), channel_id=1, replica_groups=mesh['row'=8,'col'=32] {'row'}, dimensions={0} | all-to-all | bytes 524288 | tf_op jit(solution)/shard_map/all_to_all | solution.py:221
  105.8 4.2 %conditional.14 = (bf16[4,16,128]{2,1,0:T(8,128)(2,1)S(1)}) conditional(s32[]{:T(128)} %bitcast.8, bf16[4,16,128]{2,1,0:T(8,128)(2,1)S(1)} %pad_maximum_fusion.1, bf16[4,16,128]{2,1,0:T(8,128)(2,1)S(1)} %pad_maximum_fusion.1, bf16[4,16,128]{2,1,0:T(8,128)(2,1)S(1)} %pad_maximum_fusion.1, ...), branch_computations={%region_29.30_spmd, %region_30.31_spmd, %region_31.32_spmd, %regio... | conditional | bytes 98352 | solution.py:37
  105.8 3.0 %collective-permute-start.19 = (bf16[4,16,128]{2,1,0:T(8,128)(2,1)S(1)}, bf16[4,16,128]{2,1,0:T(8,128)(2,1)S(1)}, u32[]{:S(2)}, u32[]{:S(2)}) collective-permute-start(bf16[4,16,128]{2,1,0:T(8,128)(2,1)S(1)} %param.26), channel_id=1, source_target_pairs={{0,16},{1,17},{2,18},{3,19},{4,20},{5,21},{6,22},{7,23},{8,24},{9,... | collective-permute-start | bytes 49160 | tf_op jit(solution)/shard_map/cond/branch_2_fun/ppermute | solution.py:24
  110.0 2.6 %conditional.15 = (bf16[4,16,128]{2,1,0:T(8,128)(2,1)S(1)}) conditional(s32[]{:T(128)} %bitcast.7, bf16[4,16,128]{2,1,0:T(8,128)(2,1)S(1)} %get-tuple-element.215, bf16[4,16,128]{2,1,0:T(8,128)(2,1)S(1)} %get-tuple-element.215, bf16[4,16,128]{2,1,0:T(8,128)(2,1)S(1)} %get-tuple-element.215, ...), branch_computations={%region_33.34_spmd, %region_34.35_spmd, %region_35.36_spmd, %regio... | conditional | bytes 98352 | solution.py:37
  110.0 2.6 %collective-permute-done.21 = bf16[4,16,128]{2,1,0:T(8,128)(2,1)S(1)} collective-permute-done((bf16[4,16,128]{2,1,0:T(8,128)(2,1)S(1)}, bf16[4,16,128]{2,1,0:T(8,128)(2,1)S(1)}, u32[]{:S(2)}, u32[]{:S(2)}) %collective-permute-start.21) | collective-permute-done | bytes 16416 | tf_op jit(solution)/shard_map/cond/branch_1_fun/ppermute | solution.py:24
  114.3 3.4 %all-to-all-start.4 = ((f32[8,8,1024]{2,1,0:T(8,128)}), f32[8,8,1024]{2,1,0:T(8,128)S(1)}, u32[]{:S(2)}, u32[]{:S(2)}) async-start(f32[8,8,1024]{2,1,0:T(8,128)} %shard_map.59), calls=%async_computation.4 | async-start | bytes 524288 | tf_op jit(solution)/shard_map/all_to_all | solution.py:221
  117.7 9.4 %all-to-all-done.4 = f32[8,8,1024]{2,1,0:T(8,128)S(1)} async-done(((f32[8,8,1024]{2,1,0:T(8,128)}), f32[8,8,1024]{2,1,0:T(8,128)S(1)}, u32[]{:S(2)}, u32[]{:S(2)}) %all-to-all-start.4) | async-done | bytes 262176 | tf_op jit(solution)/shard_map/all_to_all | solution.py:221
  128.4 3.4 %collective-permute-start.33 = (f32[8,128]{1,0:T(8,128)S(1)}, f32[8,128]{1,0:T(8,128)S(1)}, u32[]{:S(2)}, u32[]{:S(2)}) collective-permute-start(f32[8,128]{1,0:T(8,128)S(1)} %fusion), channel_id=1, source_target_pairs={{0,1},{1,0},{2,3},{3,2},{4,5},{5,4},{6,7},{7,6},{8,9},{9,8},{10,11... | collective-permute-start | bytes 12296 | tf_op jit(solution)/shard_map/ppermute | solution.py:24
  132.8 15.1 %all_to_all.38.sent_ref = bf16[16,5,16,128]{3,2,1,0:T(8,128)(2,1)S(1)} all-to-all(bf16[16,5,16,128]{3,2,1,0:T(8,128)(2,1)S(1)} %broadcast_in_dim.130), channel_id=1, replica_groups={{0,2,4,6,8,10,12,14,16,18,20,22,24,26,28,30},{1,3,5,7,9,11,13,15,17,19,..., dimensions={0} | all-to-all | bytes 655360 | tf_op jit(solution)/shard_map/all_to_all | solution.py:19
  150.5 2.7 %shard_map.60 = f32[8,4,16,128]{3,2,1,0:T(8,128)S(1)} custom-call(s32[13]{0:T(128)S(1)} %concatenate.159.at_ref, bf16[16,5,16,128]{3,2,1,0:T(8,128)(2,1)S(1)} %all_to_all.38.sent_ref, bf16[5,4096,128]{2,1,0:T(8,128)(2,1)S(1)} %bitcast.77), custom_call_target="tpu_custom_call" | custom-call | flops 83886080 | bytes 5242880 | tf_op jit(solution)/shard_map/pallas_call | solution.py:141
  153.2 12.6 %all_to_all.39 = f32[8,4,16,128]{3,2,1,0:T(8,128)S(1)} all-to-all(f32[8,4,16,128]{3,2,1,0:T(8,128)S(1)} %shard_map.60), channel_id=1, replica_groups=mesh['row'=8,'col'=32] {'row'}, dimensions={0} | all-to-all | bytes 524288 | tf_op jit(solution)/shard_map/all_to_all | solution.py:244
  (94 shorter events, 44.2 us)
Async XLA Ops:
  2.3 9.7 %collective-permute-start.24 = (f32[5,16,128]{2,1,0:T(8,128)S(1)}, f32[5,16,128]{2,1,0:T(8,128)S(1)}, u32[]{:S(2)}, u32[]{:S(2)}) collective-permute-start(f32[5,16,128]{2,1,0:T(8,128)S(1)} %select_reduce_fusion.1.own_side), channel_id=1, source_target_pairs={{0,1},{1,0},{2,3},{3,2},{4,5},{5,4},{6,7},{7,6},{8,9},{9,8},{10,11... | collective-permute-start | bytes 122888 | tf_op jit(solution)/shard_map/ppermute | solution.py:24
  6.8 2.5 %copy-start = (bf16[4096,5,128]{2,0,1:T(8,128)(2,1)S(1)}, bf16[4096,5,128]{2,0,1:T(8,128)(2,1)}, u32[]{:S(2)}) copy-start(bf16[4096,5,128]{2,0,1:T(8,128)(2,1)} %param.37) | copy-start | bytes 15728644
  9.3 2.5 %copy-start.4 = (s32[16]{0:T(128)S(1)}, s32[16]{0:T(128)}, u32[]{:S(2)}) copy-start(s32[16]{0:T(128)} %param.41) | copy-start | bytes 196
  10.7 15.2 %collective-permute-start.25 = (bf16[1,1024,128]{2,1,0:T(8,128)(2,1)}, bf16[1,1024,128]{2,1,0:T(8,128)(2,1)}, u32[]{:S(2)}, u32[]{:S(2)}) collective-permute-start(bf16[1,1024,128]{2,1,0:T(8,128)(2,1)} %get-tuple-element.139.own_ref), channel_id=1, source_target_pairs={{0,1},{1,0},{2,3},{3,2},{4,5},{5,4},{6,7},{7,6},{8,9},{9,8},{10,11... | collective-permute-start | bytes 786440 | tf_op jit(solution)/shard_map/ppermute | solution.py:24
  10.7 15.2 %collective-permute-start.26 = (bf16[2,1024,128]{2,1,0:T(8,128)(2,1)S(1)}, bf16[2,1024,128]{2,1,0:T(8,128)(2,1)}, u32[]{:S(2)}, u32[]{:S(2)}) collective-permute-start(bf16[2,1024,128]{2,1,0:T(8,128)(2,1)S(1)} %get-tuple-element.148.own_ref), channel_id=1, source_target_pairs={{0,1},{1,0},{2,3},{3,2},{4,5},{5,4},{6,7},{7,6},{8,9},{9,8},{10,11... | collective-permute-start | bytes 1572872 | tf_op jit(solution)/shard_map/ppermute | solution.py:24
  11.2 14.7 %collective-permute-start.27 = (bf16[3,1024,128]{2,1,0:T(8,128)(2,1)S(1)}, bf16[3,1024,128]{2,1,0:T(8,128)(2,1)}, u32[]{:S(2)}, u32[]{:S(2)}) collective-permute-start(bf16[3,1024,128]{2,1,0:T(8,128)(2,1)S(1)} %get-tuple-element.157.own_ref), channel_id=1, source_target_pairs={{0,1},{1,0},{2,3},{3,2},{4,5},{5,4},{6,7},{7,6},{8,9},{9,8},{10,11... | collective-permute-start | bytes 2359304 | tf_op jit(solution)/shard_map/ppermute | solution.py:24
  11.2 14.7 %collective-permute-start.28 = (bf16[4,1024,128]{2,1,0:T(8,128)(2,1)S(1)}, bf16[4,1024,128]{2,1,0:T(8,128)(2,1)S(1)}, u32[]{:S(2)}, u32[]{:S(2)}) collective-permute-start(bf16[4,1024,128]{2,1,0:T(8,128)(2,1)S(1)} %get-tuple-element.168.own_ref), channel_id=1, source_target_pairs={{0,1},{1,0},{2,3},{3,2},{4,5},{5,4},{6,7},{7,6},{8,9},{9,8},{10,11... | collective-permute-start | bytes 3145736 | tf_op jit(solution)/shard_map/ppermute | solution.py:24
  12.6 13.4 %all-to-all-start = ((f32[8,8,128]{2,1,0:T(8,128)}), f32[8,8,128]{2,1,0:T(8,128)S(1)}, u32[]{:S(2)}, u32[]{:S(2)}) async-start(f32[8,8,128]{2,1,0:T(8,128)} %broadcast_in_dim.118), calls=%async_computation | async-start | bytes 65536 | tf_op jit(solution)/shard_map/all_to_all | solution.py:19
  27.2 2.3 %collective-permute-start.29 = (f32[8,128]{1,0:T(8,128)S(1)}, f32[8,128]{1,0:T(8,128)S(1)}, u32[]{:S(2)}, u32[]{:S(2)}) collective-permute-start(f32[8,128]{1,0:T(8,128)S(1)} %fusion.8), channel_id=1, source_target_pairs={{0,1},{1,0},{2,3},{3,2},{4,5},{5,4},{6,7},{7,6},{8,9},{9,8},{10,11... | collective-permute-start | bytes 12296 | tf_op jit(solution)/shard_map/ppermute | solution.py:24
  29.6 4.0 %collective-permute-start.1 = (bf16[1,16,128]{2,1,0:T(8,128)(2,1)S(1)}, bf16[1,16,128]{2,1,0:T(8,128)(2,1)S(1)}, u32[]{:S(2)}, u32[]{:S(2)}) collective-permute-start(bf16[1,16,128]{2,1,0:T(8,128)(2,1)S(1)} %param.2), channel_id=1, source_target_pairs={{0,16},{1,17},{2,18},{3,19},{4,20},{5,21},{6,22},{7,23},{8,24},{9,... | collective-permute-start | bytes 12296 | tf_op jit(solution)/shard_map/cond/branch_2_fun/ppermute | solution.py:24
  51.0 3.9 %collective-permute-start.30 = (f32[8,128]{1,0:T(8,128)S(1)}, f32[8,128]{1,0:T(8,128)S(1)}, u32[]{:S(2)}, u32[]{:S(2)}) collective-permute-start(f32[8,128]{1,0:T(8,128)S(1)} %fusion.6), channel_id=1, source_target_pairs={{0,1},{1,0},{2,3},{3,2},{4,5},{5,4},{6,7},{7,6},{8,9},{9,8},{10,11... | collective-permute-start | bytes 12296 | tf_op jit(solution)/shard_map/ppermute | solution.py:24
  55.7 2.6 %collective-permute-start.6 = (bf16[2,16,128]{2,1,0:T(8,128)(2,1)S(1)}, bf16[2,16,128]{2,1,0:T(8,128)(2,1)S(1)}, u32[]{:S(2)}, u32[]{:S(2)}) collective-permute-start(bf16[2,16,128]{2,1,0:T(8,128)(2,1)S(1)} %param.9), channel_id=1, source_target_pairs={{0,8},{1,9},{2,10},{3,11},{4,12},{5,13},{6,14},{7,15},{8,0},{9,1},... | collective-permute-start | bytes 24584 | tf_op jit(solution)/shard_map/cond/branch_1_fun/ppermute | solution.py:24
  58.2 23.6 %copy-start.3 = (pred[16]{0:T(512)(128)(4,1)S(1)}, pred[16]{0:T(512)(128)(4,1)}, u32[]{:S(2)}) copy-start(pred[16]{0:T(512)(128)(4,1)} %get-tuple-element.190) | copy-start | bytes 52
  58.2 4.0 %collective-permute-start.10 = (bf16[2,16,128]{2,1,0:T(8,128)(2,1)S(1)}, bf16[2,16,128]{2,1,0:T(8,128)(2,1)S(1)}, u32[]{:S(2)}, u32[]{:S(2)}) collective-permute-start(bf16[2,16,128]{2,1,0:T(8,128)(2,1)S(1)} %param.14), channel_id=1, source_target_pairs={{0,4},{1,5},{2,6},{3,7},{4,0},{5,1},{6,2},{7,3},{8,12},{9,13},{10,... | collective-permute-start | bytes 24584 | tf_op jit(solution)/shard_map/cond/branch_2_fun/ppermute | solution.py:24
  77.3 4.6 %collective-permute-start.31 = (f32[8,128]{1,0:T(8,128)S(1)}, f32[8,128]{1,0:T(8,128)S(1)}, u32[]{:S(2)}, u32[]{:S(2)}) collective-permute-start(f32[8,128]{1,0:T(8,128)S(1)} %fusion.4), channel_id=1, source_target_pairs={{0,1},{1,0},{2,3},{3,2},{4,5},{5,4},{6,7},{7,6},{8,9},{9,8},{10,11... | collective-permute-start | bytes 12296 | tf_op jit(solution)/shard_map/ppermute | solution.py:24
  82.0 3.8 %collective-permute-start.17 = (bf16[3,16,128]{2,1,0:T(8,128)(2,1)S(1)}, bf16[3,16,128]{2,1,0:T(8,128)(2,1)S(1)}, u32[]{:S(2)}, u32[]{:S(2)}) collective-permute-start(bf16[3,16,128]{2,1,0:T(8,128)(2,1)S(1)} %param.23), channel_id=1, source_target_pairs={{0,6},{1,7},{2,4},{3,5},{4,2},{5,3},{6,0},{7,1},{8,14},{9,15},{10,... | collective-permute-start | bytes 36872 | tf_op jit(solution)/shard_map/cond/branch_3_fun/ppermute | solution.py:24
  101.9 3.8 %collective-permute-start.32 = (f32[8,128]{1,0:T(8,128)S(1)}, f32[8,128]{1,0:T(8,128)S(1)}, u32[]{:S(2)}, u32[]{:S(2)}) collective-permute-start(f32[8,128]{1,0:T(8,128)S(1)} %fusion.2), channel_id=1, source_target_pairs={{0,1},{1,0},{2,3},{3,2},{4,5},{5,4},{6,7},{7,6},{8,9},{9,8},{10,11... | collective-permute-start | bytes 12296 | tf_op jit(solution)/shard_map/ppermute | solution.py:24
  105.8 4.2 %collective-permute-start.19 = (bf16[4,16,128]{2,1,0:T(8,128)(2,1)S(1)}, bf16[4,16,128]{2,1,0:T(8,128)(2,1)S(1)}, u32[]{:S(2)}, u32[]{:S(2)}) collective-permute-start(bf16[4,16,128]{2,1,0:T(8,128)(2,1)S(1)} %param.26), channel_id=1, source_target_pairs={{0,16},{1,17},{2,18},{3,19},{4,20},{5,21},{6,22},{7,23},{8,24},{9,... | collective-permute-start | bytes 49160 | tf_op jit(solution)/shard_map/cond/branch_2_fun/ppermute | solution.py:24
  110.0 2.6 %collective-permute-start.21 = (bf16[4,16,128]{2,1,0:T(8,128)(2,1)S(1)}, bf16[4,16,128]{2,1,0:T(8,128)(2,1)S(1)}, u32[]{:S(2)}, u32[]{:S(2)}) collective-permute-start(bf16[4,16,128]{2,1,0:T(8,128)(2,1)S(1)} %param.29), channel_id=1, source_target_pairs={{0,2},{1,3},{2,0},{3,1},{4,6},{5,7},{6,4},{7,5},{8,10},{9,11},{10,... | collective-permute-start | bytes 49160 | tf_op jit(solution)/shard_map/cond/branch_1_fun/ppermute | solution.py:24
  114.3 12.8 %all-to-all-start.4 = ((f32[8,8,1024]{2,1,0:T(8,128)}), f32[8,8,1024]{2,1,0:T(8,128)S(1)}, u32[]{:S(2)}, u32[]{:S(2)}) async-start(f32[8,8,1024]{2,1,0:T(8,128)} %shard_map.59), calls=%async_computation.4 | async-start | bytes 524288 | tf_op jit(solution)/shard_map/all_to_all | solution.py:221
  128.4 4.2 %collective-permute-start.33 = (f32[8,128]{1,0:T(8,128)S(1)}, f32[8,128]{1,0:T(8,128)S(1)}, u32[]{:S(2)}, u32[]{:S(2)}) collective-permute-start(f32[8,128]{1,0:T(8,128)S(1)} %fusion), channel_id=1, source_target_pairs={{0,1},{1,0},{2,3},{3,2},{4,5},{5,4},{6,7},{7,6},{8,9},{9,8},{10,11... | collective-permute-start | bytes 12296 | tf_op jit(solution)/shard_map/ppermute | solution.py:24
  148.0 2.5 %copy-start.1 = (bf16[4096,5,128]{2,0,1:T(8,128)(2,1)S(1)}, bf16[4096,5,128]{2,0,1:T(8,128)(2,1)}, u32[]{:S(2)}) copy-start(bf16[4096,5,128]{2,0,1:T(8,128)(2,1)} %param.37) | copy-start | bytes 15728644
  150.5 15.4 %copy-start.2 = (f32[16,4,128]{2,1,0:T(4,128)S(1)}, f32[16,4,128]{2,1,0:T(4,128)}, u32[]{:S(2)}) copy-start(f32[16,4,128]{2,1,0:T(4,128)} %param.39) | copy-start | bytes 98308
where the time goes:
time: 168 us; the launch traced here: 167 us
  blocking collectives  65.7 us (39%)
  starting transfers between devices  40.3 us (24%)
  waiting for transfers between devices  23.8 us (14%)
  Pallas kernels  11.6 us (7%)
  local copies, waits for them, and re-layouts  8.99 us (5%)
  matrix products  6.26 us (4%)
  between operations  5.79 us (3%)
  other arithmetic  4.04 us (2%)
    all_to_all x3, blocking collectives, per_device(): remaining = lax.all_to_all(copies, 'row', 0, 0, tiled=True).sum(axis=0)  37.9 us
    ppermute x16, starting transfers between devices, from_mask(): return lax.ppermute(array, 'col', [(i, i ^ mask) for i in range(size)])  30.4 us
    all_to_all x1, blocking collectives, to_all(): lax.all_to_all(copies, axis, 0, 0, axis_index_groups=groups, tiled=True)  15.1 us
    all_to_all x1, blocking collectives, per_device(): total = lax.all_to_all(pieces, 'row', 0, 0, tiled=True).sum(axis=0)  12.6 us
    ppermute x16, waiting for transfers between devices, from_mask(): return lax.ppermute(array, 'col', [(i, i ^ mask) for i in range(size)])  9.61 us
    all_to_all x1, waiting for transfers between devices, per_device(): remaining = lax.all_to_all(copies, 'row', 0, 0, tiled=True).sum(axis=0)  9.36 us
    pallas_call x4, Pallas kernels, partial_half(): pl.pallas_call(functools.partial(partial_kernel, section), out_shape=jax....  7.39 us
    all_to_all x1, starting transfers between devices, to_all(): lax.all_to_all(copies, axis, 0, 0, axis_index_groups=groups, tiled=True)  6.48 us
  transfers between devices with their start and end apart: 18, of which 10 were waited for; matrix products, arithmetic and copies ran while one was open for 2% of the time, Pallas kernels for 1%

commit v1 on v0

--- a/solution.py
+++ b/solution.py
@@ -181,7 +181,7 @@
         return jnp.where(core == 0, array[:half], array[half:])
 
     other_sides = from_mask(sides, 1)
-    share = own_half(jnp.where(mine[0], sides[0], other_sides[0]))
+    share = own_half(jnp.where(mine[:, None, None], sides, other_sides)[0])
     arrived = to_all(share, "row", peers)
 
     chip = lax.shift_right_logical(owner[-1], jnp.int32(1))
@@ -196,6 +196,7 @@
     ]
     live = order[:, None] < live_segments[None, :]
     taken = (here & mine[:, None])[:, None, :] & live[:, :, None]
+    live = jnp.broadcast_to(live[:, :, None].astype(F32), sides.shape)
     done = taken.any(axis=0)[:, :, None]
     first = (arrived, at, live, taken, done, sides, other_sides, own_rows, other_rows)
     arrived, at, live, taken, done, sides, other_sides, own_rows, other_rows = (
@@ -231,7 +232,7 @@
             core == 0, jnp.concatenate([solved, other]), jnp.concatenate([other, solved])
         )
         solves.append(solved)
-        sent = jnp.where(live[section][:, None], solved, 0.0).astype(BF16)[None]
+        sent = jnp.where(live[section] > 0, solved, 0.0).astype(BF16)[None]
         history = sent if history is None else jnp.concatenate([history, sent])
         if section < section_count - 1:
             history, solves = lax.optimization_barrier((history, solves))

time: 168 us -> 171 us (1.018)
    all_to_all x1, waiting for transfers between devices: 4.87 us -> 6.8 us  [to_all(): lax.all_to_all(copies, axis, 0, 0, axis_index_groups=groups, tiled=True)]
    unnamed x15 -> x21, local copies, waits for them, and re-layouts: 5.76 us -> 6.36 us
  transfers between devices with their start and end apart: 18 -> 18, of which waited for: 10 -> 9; matrix products, arithmetic and copies ran while one was open for 2% -> 2% of each run, Pallas kernels for 1% -> 1%
where the time goes in v1:
time: 171 us; the launch traced here: 170 us
  blocking collectives  65.8 us (38%)
  starting transfers between devices  40.1 us (23%)
  waiting for transfers between devices  25.5 us (15%)
  Pallas kernels  11.6 us (7%)
  local copies, waits for them, and re-layouts  9.06 us (5%)
  matrix products  6.3 us (4%)
  between operations  5.94 us (3%)
  other arithmetic  5.35 us (3%)
    all_to_all x3, blocking collectives, per_device(): remaining = lax.all_to_all(copies, 'row', 0, 0, tiled=True).sum(axis=0)  38 us
    ppermute x16, starting transfers between devices, from_mask(): return lax.ppermute(array, 'col', [(i, i ^ mask) for i in range(size)])  30.2 us
    all_to_all x1, blocking collectives, to_all(): lax.all_to_all(copies, axis, 0, 0, axis_index_groups=groups, tiled=True)  15.1 us
    all_to_all x1, blocking collectives, per_device(): total = lax.all_to_all(pieces, 'row', 0, 0, tiled=True).sum(axis=0)  12.6 us
    ppermute x16, waiting for transfers between devices, from_mask(): return lax.ppermute(array, 'col', [(i, i ^ mask) for i in range(size)])  9.4 us
    all_to_all x1, waiting for transfers between devices, per_device(): remaining = lax.all_to_all(copies, 'row', 0, 0, tiled=True).sum(axis=0)  9.35 us
    pallas_call x4, Pallas kernels, partial_half(): pl.pallas_call(functools.partial(partial_kernel, section), out_shape=jax....  7.39 us
    all_to_all x1, waiting for transfers between devices, to_all(): lax.all_to_all(copies, axis, 0, 0, axis_index_groups=groups, tiled=True)  6.8 us
  transfers between devices with their start and end apart: 18, of which 9 were waited for; matrix products, arithmetic and copies ran while one was open for 2% of the time, Pallas kernels for 1%

profile of v1, /device:TPU:1, one launch (start us, length us, event | category | flops | bytes accessed | tf_op | source)
XLA Modules:
  0.0 169.8 jit_solution(16968785810978511477)
XLA Ops:
  2.3 3.3 %collective-permute-start.24 = (f32[5,16,128]{2,1,0:T(8,128)S(1)}, f32[5,16,128]{2,1,0:T(8,128)S(1)}, u32[]{:S(2)}, u32[]{:S(2)}) collective-permute-start(f32[5,16,128]{2,1,0:T(8,128)S(1)} %select_reduce_fusion.1.own_side), channel_id=1, source_target_pairs={{0,1},{1,0},{2,3},{3,2},{4,5},{5,4},{6,7},{7,6},{8,9},{9,8},{10,11... | collective-permute-start | bytes 122888 | tf_op jit(solution)/shard_map/ppermute | solution.py:24
  13.6 6.5 %all-to-all-start = ((f32[8,8,128]{2,1,0:T(8,128)}), f32[8,8,128]{2,1,0:T(8,128)S(1)}, u32[]{:S(2)}, u32[]{:S(2)}) async-start(f32[8,8,128]{2,1,0:T(8,128)} %broadcast_in_dim.107), calls=%async_computation | async-start | bytes 65536 | tf_op jit(solution)/shard_map/all_to_all | solution.py:19
  20.2 6.8 %all-to-all-done = f32[8,8,128]{2,1,0:T(8,128)S(1)} async-done(((f32[8,8,128]{2,1,0:T(8,128)}), f32[8,8,128]{2,1,0:T(8,128)S(1)}, u32[]{:S(2)}, u32[]{:S(2)}) %all-to-all-start) | async-done | bytes 32800 | tf_op jit(solution)/shard_map/all_to_all | solution.py:19
  32.4 4.1 %conditional.8 = (bf16[1,16,128]{2,1,0:T(8,128)(2,1)S(1)}) conditional(s32[]{:T(128)} %bitcast.13, bf16[1,16,128]{2,1,0:T(8,128)(2,1)S(1)} %fusion.18, bf16[1,16,128]{2,1,0:T(8,128)(2,1)S(1)} %fusion.18, bf16[1,16,128]{2,1,0:T(8,128)(2,1)S(1)} %fusion.18, bf16[1,16,128]{2,1,0:T(8,128)(2,1)S(1)} %fusion.18), branch_computations={%region_2.3_spmd, %region_3.4_spmd, %region_4.5_spmd, %region_5.6_... | conditional | bytes 24624 | solution.py:37
  32.4 3.0 %collective-permute-start.1 = (bf16[1,16,128]{2,1,0:T(8,128)(2,1)S(1)}, bf16[1,16,128]{2,1,0:T(8,128)(2,1)S(1)}, u32[]{:S(2)}, u32[]{:S(2)}) collective-permute-start(bf16[1,16,128]{2,1,0:T(8,128)(2,1)S(1)} %param.2), channel_id=1, source_target_pairs={{0,16},{1,17},{2,18},{3,19},{4,20},{5,21},{6,22},{7,23},{8,24},{9,... | collective-permute-start | bytes 12296 | tf_op jit(solution)/shard_map/cond/branch_2_fun/ppermute | solution.py:24
  38.3 13.4 %all_to_all.35 = f32[8,8,1024]{2,1,0:T(8,128)} all-to-all(f32[8,8,1024]{2,1,0:T(8,128)S(1)} %shard_map.56), channel_id=1, replica_groups=mesh['row'=8,'col'=32] {'row'}, dimensions={0} | all-to-all | bytes 524288 | tf_op jit(solution)/shard_map/all_to_all | solution.py:222
  61.4 4.0 %conditional.11 = (bf16[2,16,128]{2,1,0:T(8,128)(2,1)S(1)}) conditional(s32[]{:T(128)} %bitcast.10, bf16[2,16,128]{2,1,0:T(8,128)(2,1)S(1)} %get-tuple-element.208, bf16[2,16,128]{2,1,0:T(8,128)(2,1)S(1)} %get-tuple-element.208, bf16[2,16,128]{2,1,0:T(8,128)(2,1)S(1)} %get-tuple-element.208, ...), branch_computations={%region_15.16_spmd, %region_16.17_spmd, %region_17.18_spmd, %regio... | conditional | bytes 49200 | solution.py:37
  61.4 2.7 %collective-permute-start.10 = (bf16[2,16,128]{2,1,0:T(8,128)(2,1)S(1)}, bf16[2,16,128]{2,1,0:T(8,128)(2,1)S(1)}, u32[]{:S(2)}, u32[]{:S(2)}) collective-permute-start(bf16[2,16,128]{2,1,0:T(8,128)(2,1)S(1)} %param.14), channel_id=1, source_target_pairs={{0,4},{1,5},{2,6},{3,7},{4,0},{5,1},{6,2},{7,3},{8,12},{9,13},{10,... | collective-permute-start | bytes 24584 | tf_op jit(solution)/shard_map/cond/branch_2_fun/ppermute | solution.py:24
  67.3 11.9 %all_to_all.36 = f32[8,8,1024]{2,1,0:T(8,128)S(1)} all-to-all(f32[8,8,1024]{2,1,0:T(8,128)S(1)} %shard_map.57), channel_id=1, replica_groups=mesh['row'=8,'col'=32] {'row'}, dimensions={0} | all-to-all | bytes 524288 | tf_op jit(solution)/shard_map/all_to_all | solution.py:222
  80.5 3.4 %collective-permute-start.31 = (f32[8,128]{1,0:T(8,128)S(1)}, f32[8,128]{1,0:T(8,128)S(1)}, u32[]{:S(2)}, u32[]{:S(2)}) collective-permute-start(f32[8,128]{1,0:T(8,128)S(1)} %fusion.4), channel_id=1, source_target_pairs={{0,1},{1,0},{2,3},{3,2},{4,5},{5,4},{6,7},{7,6},{8,9},{9,8},{10,11... | collective-permute-start | bytes 12296 | tf_op jit(solution)/shard_map/ppermute | solution.py:24
  85.2 3.9 %conditional.13 = (bf16[3,16,128]{2,1,0:T(8,128)(2,1)S(1)}) conditional(s32[]{:T(128)} %bitcast.8, bf16[3,16,128]{2,1,0:T(8,128)(2,1)S(1)} %get-tuple-element.210, bf16[3,16,128]{2,1,0:T(8,128)(2,1)S(1)} %get-tuple-element.210, bf16[3,16,128]{2,1,0:T(8,128)(2,1)S(1)} %get-tuple-element.210, ...), branch_computations={%region_24.25_spmd, %region_25.26_spmd, %region_26.27_spmd, %regio... | conditional | bytes 73776 | solution.py:37
  85.2 2.6 %collective-permute-start.17 = (bf16[3,16,128]{2,1,0:T(8,128)(2,1)S(1)}, bf16[3,16,128]{2,1,0:T(8,128)(2,1)S(1)}, u32[]{:S(2)}, u32[]{:S(2)}) collective-permute-start(bf16[3,16,128]{2,1,0:T(8,128)(2,1)S(1)} %param.23), channel_id=1, source_target_pairs={{0,6},{1,7},{2,4},{3,5},{4,2},{5,3},{6,0},{7,1},{8,14},{9,15},{10,... | collective-permute-start | bytes 36872 | tf_op jit(solution)/shard_map/cond/branch_3_fun/ppermute | solution.py:24
  91.1 12.7 %all_to_all.37 = f32[8,8,1024]{2,1,0:T(8,128)S(1)} all-to-all(f32[8,8,1024]{2,1,0:T(8,128)S(1)} %shard_map.58), channel_id=1, replica_groups=mesh['row'=8,'col'=32] {'row'}, dimensions={0} | all-to-all | bytes 524288 | tf_op jit(solution)/shard_map/all_to_all | solution.py:222
  105.1 2.5 %collective-permute-start.32 = (f32[8,128]{1,0:T(8,128)S(1)}, f32[8,128]{1,0:T(8,128)S(1)}, u32[]{:S(2)}, u32[]{:S(2)}) collective-permute-start(f32[8,128]{1,0:T(8,128)S(1)} %fusion.2), channel_id=1, source_target_pairs={{0,1},{1,0},{2,3},{3,2},{4,5},{5,4},{6,7},{7,6},{8,9},{9,8},{10,11... | collective-permute-start | bytes 12296 | tf_op jit(solution)/shard_map/ppermute | solution.py:24
  109.0 4.2 %conditional.14 = (bf16[4,16,128]{2,1,0:T(8,128)(2,1)S(1)}) conditional(s32[]{:T(128)} %bitcast.7, bf16[4,16,128]{2,1,0:T(8,128)(2,1)S(1)} %pad_maximum_fusion.1, bf16[4,16,128]{2,1,0:T(8,128)(2,1)S(1)} %pad_maximum_fusion.1, bf16[4,16,128]{2,1,0:T(8,128)(2,1)S(1)} %pad_maximum_fusion.1, ...), branch_computations={%region_29.30_spmd, %region_30.31_spmd, %region_31.32_spmd, %regio... | conditional | bytes 98352 | solution.py:37
  109.1 3.0 %collective-permute-start.19 = (bf16[4,16,128]{2,1,0:T(8,128)(2,1)S(1)}, bf16[4,16,128]{2,1,0:T(8,128)(2,1)S(1)}, u32[]{:S(2)}, u32[]{:S(2)}) collective-permute-start(bf16[4,16,128]{2,1,0:T(8,128)(2,1)S(1)} %param.26), channel_id=1, source_target_pairs={{0,16},{1,17},{2,18},{3,19},{4,20},{5,21},{6,22},{7,23},{8,24},{9,... | collective-permute-start | bytes 49160 | tf_op jit(solution)/shard_map/cond/branch_2_fun/ppermute | solution.py:24
  113.2 2.6 %conditional.15 = (bf16[4,16,128]{2,1,0:T(8,128)(2,1)S(1)}) conditional(s32[]{:T(128)} %bitcast.6, bf16[4,16,128]{2,1,0:T(8,128)(2,1)S(1)} %get-tuple-element.212, bf16[4,16,128]{2,1,0:T(8,128)(2,1)S(1)} %get-tuple-element.212, bf16[4,16,128]{2,1,0:T(8,128)(2,1)S(1)} %get-tuple-element.212, ...), branch_computations={%region_33.34_spmd, %region_34.35_spmd, %region_35.36_spmd, %regio... | conditional | bytes 98352 | solution.py:37
  113.2 2.6 %collective-permute-done.21 = bf16[4,16,128]{2,1,0:T(8,128)(2,1)S(1)} collective-permute-done((bf16[4,16,128]{2,1,0:T(8,128)(2,1)S(1)}, bf16[4,16,128]{2,1,0:T(8,128)(2,1)S(1)}, u32[]{:S(2)}, u32[]{:S(2)}) %collective-permute-start.21) | collective-permute-done | bytes 16416 | tf_op jit(solution)/shard_map/cond/branch_1_fun/ppermute | solution.py:24
  117.5 3.4 %all-to-all-start.4 = ((f32[8,8,1024]{2,1,0:T(8,128)}), f32[8,8,1024]{2,1,0:T(8,128)S(1)}, u32[]{:S(2)}, u32[]{:S(2)}) async-start(f32[8,8,1024]{2,1,0:T(8,128)} %shard_map.59), calls=%async_computation.4 | async-start | bytes 524288 | tf_op jit(solution)/shard_map/all_to_all | solution.py:222
  121.0 9.4 %all-to-all-done.4 = f32[8,8,1024]{2,1,0:T(8,128)S(1)} async-done(((f32[8,8,1024]{2,1,0:T(8,128)}), f32[8,8,1024]{2,1,0:T(8,128)S(1)}, u32[]{:S(2)}, u32[]{:S(2)}) %all-to-all-start.4) | async-done | bytes 262176 | tf_op jit(solution)/shard_map/all_to_all | solution.py:222
  131.6 3.4 %collective-permute-start.33 = (f32[8,128]{1,0:T(8,128)S(1)}, f32[8,128]{1,0:T(8,128)S(1)}, u32[]{:S(2)}, u32[]{:S(2)}) collective-permute-start(f32[8,128]{1,0:T(8,128)S(1)} %fusion), channel_id=1, source_target_pairs={{0,1},{1,0},{2,3},{3,2},{4,5},{5,4},{6,7},{7,6},{8,9},{9,8},{10,11... | collective-permute-start | bytes 12296 | tf_op jit(solution)/shard_map/ppermute | solution.py:24
  136.0 15.1 %all_to_all.38.sent_ref = bf16[16,5,16,128]{3,2,1,0:T(8,128)(2,1)S(1)} all-to-all(bf16[16,5,16,128]{3,2,1,0:T(8,128)(2,1)S(1)} %broadcast_in_dim.114), channel_id=1, replica_groups={{0,2,4,6,8,10,12,14,16,18,20,22,24,26,28,30},{1,3,5,7,9,11,13,15,17,19,..., dimensions={0} | all-to-all | bytes 655360 | tf_op jit(solution)/shard_map/all_to_all | solution.py:19
  153.7 2.7 %shard_map.60 = f32[8,4,16,128]{3,2,1,0:T(8,128)S(1)} custom-call(s32[13]{0:T(128)S(1)} %concatenate.153.at_ref, bf16[16,5,16,128]{3,2,1,0:T(8,128)(2,1)S(1)} %all_to_all.38.sent_ref, bf16[5,4096,128]{2,1,0:T(8,128)(2,1)S(1)} %bitcast.65), custom_call_target="tpu_custom_call" | custom-call | flops 83886080 | bytes 5242880 | tf_op jit(solution)/shard_map/pallas_call | solution.py:141
  156.4 12.6 %all_to_all.39 = f32[8,4,16,128]{3,2,1,0:T(8,128)S(1)} all-to-all(f32[8,4,16,128]{3,2,1,0:T(8,128)S(1)} %shard_map.60), channel_id=1, replica_groups=mesh['row'=8,'col'=32] {'row'}, dimensions={0} | all-to-all | bytes 524288 | tf_op jit(solution)/shard_map/all_to_all | solution.py:245
  (100 shorter events, 45.2 us)
Async XLA Ops:
  2.3 10.7 %collective-permute-start.24 = (f32[5,16,128]{2,1,0:T(8,128)S(1)}, f32[5,16,128]{2,1,0:T(8,128)S(1)}, u32[]{:S(2)}, u32[]{:S(2)}) collective-permute-start(f32[5,16,128]{2,1,0:T(8,128)S(1)} %select_reduce_fusion.1.own_side), channel_id=1, source_target_pairs={{0,1},{1,0},{2,3},{3,2},{4,5},{5,4},{6,7},{7,6},{8,9},{9,8},{10,11... | collective-permute-start | bytes 122888 | tf_op jit(solution)/shard_map/ppermute | solution.py:24
  6.8 2.5 %copy-start = (bf16[4096,5,128]{2,0,1:T(8,128)(2,1)S(1)}, bf16[4096,5,128]{2,0,1:T(8,128)(2,1)}, u32[]{:S(2)}) copy-start(bf16[4096,5,128]{2,0,1:T(8,128)(2,1)} %param.37) | copy-start | bytes 15728644
  10.7 16.3 %collective-permute-start.25 = (bf16[1,1024,128]{2,1,0:T(8,128)(2,1)}, bf16[1,1024,128]{2,1,0:T(8,128)(2,1)}, u32[]{:S(2)}, u32[]{:S(2)}) collective-permute-start(bf16[1,1024,128]{2,1,0:T(8,128)(2,1)} %get-tuple-element.139.own_ref), channel_id=1, source_target_pairs={{0,1},{1,0},{2,3},{3,2},{4,5},{5,4},{6,7},{7,6},{8,9},{9,8},{10,11... | collective-permute-start | bytes 786440 | tf_op jit(solution)/shard_map/ppermute | solution.py:24
  10.7 16.3 %collective-permute-start.26 = (bf16[2,1024,128]{2,1,0:T(8,128)(2,1)S(1)}, bf16[2,1024,128]{2,1,0:T(8,128)(2,1)}, u32[]{:S(2)}, u32[]{:S(2)}) collective-permute-start(bf16[2,1024,128]{2,1,0:T(8,128)(2,1)S(1)} %get-tuple-element.148.own_ref), channel_id=1, source_target_pairs={{0,1},{1,0},{2,3},{3,2},{4,5},{5,4},{6,7},{7,6},{8,9},{9,8},{10,11... | collective-permute-start | bytes 1572872 | tf_op jit(solution)/shard_map/ppermute | solution.py:24
  11.2 15.8 %collective-permute-start.27 = (bf16[3,1024,128]{2,1,0:T(8,128)(2,1)S(1)}, bf16[3,1024,128]{2,1,0:T(8,128)(2,1)}, u32[]{:S(2)}, u32[]{:S(2)}) collective-permute-start(bf16[3,1024,128]{2,1,0:T(8,128)(2,1)S(1)} %get-tuple-element.157.own_ref), channel_id=1, source_target_pairs={{0,1},{1,0},{2,3},{3,2},{4,5},{5,4},{6,7},{7,6},{8,9},{9,8},{10,11... | collective-permute-start | bytes 2359304 | tf_op jit(solution)/shard_map/ppermute | solution.py:24
  11.3 15.8 %collective-permute-start.28 = (bf16[4,1024,128]{2,1,0:T(8,128)(2,1)S(1)}, bf16[4,1024,128]{2,1,0:T(8,128)(2,1)S(1)}, u32[]{:S(2)}, u32[]{:S(2)}) collective-permute-start(bf16[4,1024,128]{2,1,0:T(8,128)(2,1)S(1)} %get-tuple-element.168.own_ref), channel_id=1, source_target_pairs={{0,1},{1,0},{2,3},{3,2},{4,5},{5,4},{6,7},{7,6},{8,9},{9,8},{10,11... | collective-permute-start | bytes 3145736 | tf_op jit(solution)/shard_map/ppermute | solution.py:24
  13.6 13.4 %all-to-all-start = ((f32[8,8,128]{2,1,0:T(8,128)}), f32[8,8,128]{2,1,0:T(8,128)S(1)}, u32[]{:S(2)}, u32[]{:S(2)}) async-start(f32[8,8,128]{2,1,0:T(8,128)} %broadcast_in_dim.107), calls=%async_computation | async-start | bytes 65536 | tf_op jit(solution)/shard_map/all_to_all | solution.py:19
  29.0 3.4 %collective-permute-start.29 = (f32[8,128]{1,0:T(8,128)S(1)}, f32[8,128]{1,0:T(8,128)S(1)}, u32[]{:S(2)}, u32[]{:S(2)}) collective-permute-start(f32[8,128]{1,0:T(8,128)S(1)} %fusion.8), channel_id=1, source_target_pairs={{0,1},{1,0},{2,3},{3,2},{4,5},{5,4},{6,7},{7,6},{8,9},{9,8},{10,11... | collective-permute-start | bytes 12296 | tf_op jit(solution)/shard_map/ppermute | solution.py:24
  32.4 4.0 %collective-permute-start.1 = (bf16[1,16,128]{2,1,0:T(8,128)(2,1)S(1)}, bf16[1,16,128]{2,1,0:T(8,128)(2,1)S(1)}, u32[]{:S(2)}, u32[]{:S(2)}) collective-permute-start(bf16[1,16,128]{2,1,0:T(8,128)(2,1)S(1)} %param.2), channel_id=1, source_target_pairs={{0,16},{1,17},{2,18},{3,19},{4,20},{5,21},{6,22},{7,23},{8,24},{9,... | collective-permute-start | bytes 12296 | tf_op jit(solution)/shard_map/cond/branch_2_fun/ppermute | solution.py:24
  54.5 3.8 %collective-permute-start.30 = (f32[8,128]{1,0:T(8,128)S(1)}, f32[8,128]{1,0:T(8,128)S(1)}, u32[]{:S(2)}, u32[]{:S(2)}) collective-permute-start(f32[8,128]{1,0:T(8,128)S(1)} %fusion.6), channel_id=1, source_target_pairs={{0,1},{1,0},{2,3},{3,2},{4,5},{5,4},{6,7},{7,6},{8,9},{9,8},{10,11... | collective-permute-start | bytes 12296 | tf_op jit(solution)/shard_map/ppermute | solution.py:24
  58.9 2.5 %collective-permute-start.6 = (bf16[2,16,128]{2,1,0:T(8,128)(2,1)S(1)}, bf16[2,16,128]{2,1,0:T(8,128)(2,1)S(1)}, u32[]{:S(2)}, u32[]{:S(2)}) collective-permute-start(bf16[2,16,128]{2,1,0:T(8,128)(2,1)S(1)} %param.9), channel_id=1, source_target_pairs={{0,8},{1,9},{2,10},{3,11},{4,12},{5,13},{6,14},{7,15},{8,0},{9,1},... | collective-permute-start | bytes 24584 | tf_op jit(solution)/shard_map/cond/branch_1_fun/ppermute | solution.py:24
  61.4 4.0 %collective-permute-start.10 = (bf16[2,16,128]{2,1,0:T(8,128)(2,1)S(1)}, bf16[2,16,128]{2,1,0:T(8,128)(2,1)S(1)}, u32[]{:S(2)}, u32[]{:S(2)}) collective-permute-start(bf16[2,16,128]{2,1,0:T(8,128)(2,1)S(1)} %param.14), channel_id=1, source_target_pairs={{0,4},{1,5},{2,6},{3,7},{4,0},{5,1},{6,2},{7,3},{8,12},{9,13},{10,... | collective-permute-start | bytes 24584 | tf_op jit(solution)/shard_map/cond/branch_2_fun/ppermute | solution.py:24
  80.5 4.6 %collective-permute-start.31 = (f32[8,128]{1,0:T(8,128)S(1)}, f32[8,128]{1,0:T(8,128)S(1)}, u32[]{:S(2)}, u32[]{:S(2)}) collective-permute-start(f32[8,128]{1,0:T(8,128)S(1)} %fusion.4), channel_id=1, source_target_pairs={{0,1},{1,0},{2,3},{3,2},{4,5},{5,4},{6,7},{7,6},{8,9},{9,8},{10,11... | collective-permute-start | bytes 12296 | tf_op jit(solution)/shard_map/ppermute | solution.py:24
  85.2 3.8 %collective-permute-start.17 = (bf16[3,16,128]{2,1,0:T(8,128)(2,1)S(1)}, bf16[3,16,128]{2,1,0:T(8,128)(2,1)S(1)}, u32[]{:S(2)}, u32[]{:S(2)}) collective-permute-start(bf16[3,16,128]{2,1,0:T(8,128)(2,1)S(1)} %param.23), channel_id=1, source_target_pairs={{0,6},{1,7},{2,4},{3,5},{4,2},{5,3},{6,0},{7,1},{8,14},{9,15},{10,... | collective-permute-start | bytes 36872 | tf_op jit(solution)/shard_map/cond/branch_3_fun/ppermute | solution.py:24
  105.1 3.8 %collective-permute-start.32 = (f32[8,128]{1,0:T(8,128)S(1)}, f32[8,128]{1,0:T(8,128)S(1)}, u32[]{:S(2)}, u32[]{:S(2)}) collective-permute-start(f32[8,128]{1,0:T(8,128)S(1)} %fusion.2), channel_id=1, source_target_pairs={{0,1},{1,0},{2,3},{3,2},{4,5},{5,4},{6,7},{7,6},{8,9},{9,8},{10,11... | collective-permute-start | bytes 12296 | tf_op jit(solution)/shard_map/ppermute | solution.py:24
  109.1 4.2 %collective-permute-start.19 = (bf16[4,16,128]{2,1,0:T(8,128)(2,1)S(1)}, bf16[4,16,128]{2,1,0:T(8,128)(2,1)S(1)}, u32[]{:S(2)}, u32[]{:S(2)}) collective-permute-start(bf16[4,16,128]{2,1,0:T(8,128)(2,1)S(1)} %param.26), channel_id=1, source_target_pairs={{0,16},{1,17},{2,18},{3,19},{4,20},{5,21},{6,22},{7,23},{8,24},{9,... | collective-permute-start | bytes 49160 | tf_op jit(solution)/shard_map/cond/branch_2_fun/ppermute | solution.py:24
  113.2 2.6 %collective-permute-start.21 = (bf16[4,16,128]{2,1,0:T(8,128)(2,1)S(1)}, bf16[4,16,128]{2,1,0:T(8,128)(2,1)S(1)}, u32[]{:S(2)}, u32[]{:S(2)}) collective-permute-start(bf16[4,16,128]{2,1,0:T(8,128)(2,1)S(1)} %param.29), channel_id=1, source_target_pairs={{0,2},{1,3},{2,0},{3,1},{4,6},{5,7},{6,4},{7,5},{8,10},{9,11},{10,... | collective-permute-start | bytes 49160 | tf_op jit(solution)/shard_map/cond/branch_1_fun/ppermute | solution.py:24
  115.8 5.1 %copy-start.4 = (f32[16,128]{1,0:T(8,128)S(1)}, f32[16,128]{1,0:T(8,128)}, u32[]{:S(2)}) copy-start(f32[16,128]{1,0:T(8,128)} %maximum_select_fusion.3) | copy-start | bytes 24580
  115.8 20.0 %copy-start.5 = (pred[5,16,4]{1,2,0:T(4,128)(4,1)S(1)}, pred[5,16,4]{1,2,0:T(4,128)(4,1)}, u32[]{:S(2)}) copy-start(pred[5,16,4]{1,2,0:T(4,128)(4,1)} %get-tuple-element.176) | copy-start | bytes 964
  117.5 12.8 %all-to-all-start.4 = ((f32[8,8,1024]{2,1,0:T(8,128)}), f32[8,8,1024]{2,1,0:T(8,128)S(1)}, u32[]{:S(2)}, u32[]{:S(2)}) async-start(f32[8,8,1024]{2,1,0:T(8,128)} %shard_map.59), calls=%async_computation.4 | async-start | bytes 524288 | tf_op jit(solution)/shard_map/all_to_all | solution.py:222
  131.6 4.2 %collective-permute-start.33 = (f32[8,128]{1,0:T(8,128)S(1)}, f32[8,128]{1,0:T(8,128)S(1)}, u32[]{:S(2)}, u32[]{:S(2)}) collective-permute-start(f32[8,128]{1,0:T(8,128)S(1)} %fusion), channel_id=1, source_target_pairs={{0,1},{1,0},{2,3},{3,2},{4,5},{5,4},{6,7},{7,6},{8,9},{9,8},{10,11... | collective-permute-start | bytes 12296 | tf_op jit(solution)/shard_map/ppermute | solution.py:24
  151.2 2.5 %copy-start.1 = (bf16[4096,5,128]{2,0,1:T(8,128)(2,1)S(1)}, bf16[4096,5,128]{2,0,1:T(8,128)(2,1)}, u32[]{:S(2)}) copy-start(bf16[4096,5,128]{2,0,1:T(8,128)(2,1)} %param.37) | copy-start | bytes 15728644
  153.6 15.4 %copy-start.3 = (f32[16,4,128]{2,1,0:T(4,128)S(1)}, f32[16,4,128]{2,1,0:T(4,128)}, u32[]{:S(2)}) copy-start(f32[16,4,128]{2,1,0:T(4,128)} %param.39) | copy-start | bytes 98308
  153.6 15.4 %copy-start.6 = (pred[16,4]{0,1:T(4,128)(4,1)S(1)}, pred[16,4]{0,1:T(4,128)(4,1)}, u32[]{:S(2)}) copy-start(pred[16,4]{0,1:T(4,128)(4,1)} %get-tuple-element.183) | copy-start | bytes 196
  (2 other events, 3.1 us)
